TPU v7x, 32 devices: a whole 2x2x4 slice. The times are simulated.
32 devices in a mesh: energy: 8 (over y, x, core), cell: 4 (over z).
Axes of the slice: x: 2, y: 2, z: 4, core: 2. Of those that a mesh axis runs over, the one named last changes fastest.
Arguments:
- g_retarded: bfloat16 [2, 8, 4, 128, 512], P(None, 'energy', None, None, 'cell'), may hold values from -0.75 to 0.75
- sigma_lesser: bfloat16 [2, 8, 128, 512], P(None, 'energy', None, 'cell'), may hold values from -1.5 to 1.5
- w_screened: bfloat16 [2, 8, 4, 128, 512], P(None, 'energy', None, None, 'cell'), may hold values from -0.75 to 0.75
- coupling: int32 [4, 4], replicated, may hold values 0 or 1
Outputs:
- polarization: bfloat16 [4, 2, 8, 16384], P('cell', None, 'energy')
- w_lesser: bfloat16 [4, 2, 8, 128, 128], P('cell', None, 'energy')
Inputs may be any that keep to these rules, and one draw needn't show every extreme that they name: coupling[i, j] is 1 where cell i is coupled to cell j and 0 elsewhere.
All inputs are finite; a program needn't handle non-finite values.
Results may differ from a plain program's by a relative error of at most 0.024.
Values may be sent and summed in bfloat16 or wider, within the bound.
No kernel may reach another device: no remote copies, remote signals or barrier semaphores. Data moves between devices by JAX's collectives and lax.ppermute only.
A program may use at most 64 MiB of HBM per device.

v0:
```python
import math
import jax
import jax.numpy as jnp
from jax import lax
from jax.sharding import PartitionSpec as P


def forward_product(left, right):
    return jnp.einsum("eibjc,ecjd->eibjd", left, right, preferred_element_type=jnp.float32)


def adjoint_product(left, right):
    return jnp.einsum("eibjc,eidjc->iebd", left, right, preferred_element_type=jnp.float32)


def sandwich_rows(columns, sources, coupling, cell_index, count):
    orbitals = sources.shape[2]
    local_cells = sources.shape[3] // orbitals
    energies = sources.shape[1]
    rows_block = columns
    rows_block = rows_block.reshape(2, energies, count, orbitals, local_cells, orbitals)
    col_re = rows_block[0]
    col_im = rows_block[1]
    source = sources.reshape(2, energies, orbitals, local_cells, orbitals)
    src_re = source[0]
    src_im = source[1]
    mid_re = (forward_product(col_re, src_re) - forward_product(col_im, src_im)).astype(
        jnp.bfloat16
    )
    mid_im = (forward_product(col_re, src_im) + forward_product(col_im, src_re)).astype(
        jnp.bfloat16
    )
    weight = lax.dynamic_slice(coupling, (0, cell_index * local_cells), (count, local_cells))
    weight = weight.astype(jnp.bfloat16)[None, :, None, :, None]
    mid_re = mid_re * weight
    mid_im = mid_im * weight
    part_re = adjoint_product(mid_re, col_re) + adjoint_product(mid_im, col_im)
    part_im = adjoint_product(mid_im, col_re) - adjoint_product(mid_re, col_im)
    return jnp.stack([part_re, part_im], axis=1)


def correlate_spectral(spread):
    energies = spread.shape[2]
    length = 2 * energies
    freqs = jnp.arange(length, dtype=jnp.int32)[:, None]
    points = jnp.arange(energies, dtype=jnp.int32)[None, :]
    phase = jnp.mod(freqs * points, length).astype(jnp.float32) * (math.pi / energies)
    cos_table = jnp.cos(phase)
    sin_table = jnp.sin(phase)
    cos_high = cos_table.astype(jnp.bfloat16)
    cos_low = (cos_table - cos_high.astype(jnp.float32)).astype(jnp.bfloat16)
    sin_high = sin_table.astype(jnp.bfloat16)
    sin_low = (sin_table - sin_high.astype(jnp.float32)).astype(jnp.bfloat16)

    def forward(high, low, data):
        upper = jnp.einsum("ft,ctk->cfk", high, data, preferred_element_type=jnp.float32)
        return upper + jnp.einsum("ft,ctk->cfk", low, data, preferred_element_type=jnp.float32)

    def inverse(table, data):
        return jnp.einsum("ft,cfk->ctk", table, data, precision=lax.Precision.HIGH)

    low_re = spread[:, 0]
    low_im = spread[:, 1]
    high_re = spread[:, 2]
    high_im = spread[:, 3]
    spec_a_re = forward(cos_high, cos_low, low_re) + forward(sin_high, sin_low, low_im)
    spec_a_im = forward(cos_high, cos_low, low_im) - forward(sin_high, sin_low, low_re)
    spec_b_re = forward(cos_high, cos_low, high_re) + forward(sin_high, sin_low, high_im)
    spec_b_im = forward(cos_high, cos_low, high_im) - forward(sin_high, sin_low, high_re)
    cross_re = spec_a_re * spec_b_re + spec_a_im * spec_b_im
    cross_im = spec_a_im * spec_b_re - spec_a_re * spec_b_im
    back_re = (inverse(cos_table, cross_re) - inverse(sin_table, cross_im)) / length
    back_im = (inverse(cos_table, cross_im) + inverse(sin_table, cross_re)) / length
    factor = 1.0 / math.sqrt(energies)
    return jnp.stack([back_im * factor, -back_re * factor], axis=1)


def on_device(g_retarded, sigma_lesser, w_screened, coupling):
    cell_index = lax.axis_index("cell")
    orbitals = sigma_lesser.shape[2]
    local_cells = sigma_lesser.shape[3] // orbitals
    energies_dev = sigma_lesser.shape[1]
    lesser = lax.psum_scatter(
        sandwich_rows(
            g_retarded, sigma_lesser, coupling, cell_index, local_cells * lax.axis_size("cell")
        ).astype(jnp.bfloat16),
        "cell",
        scatter_dimension=0,
        tiled=True,
    ).astype(jnp.float32)
    row_block = lax.dynamic_slice_in_dim(g_retarded, cell_index * local_cells + 0, 1, 2)
    blocks = [row_block[:, :, 0, :, 0:orbitals]]
    diagonal = jnp.stack(blocks, axis=0).astype(jnp.float32)
    diag_re = diagonal[:, 0]
    diag_im = diagonal[:, 1]
    greater = lesser + jnp.stack(
        [diag_re - jnp.swapaxes(diag_re, -1, -2), diag_im + jnp.swapaxes(diag_im, -1, -2)], axis=1
    )
    both = jnp.concatenate([lesser, greater], axis=1).astype(jnp.bfloat16)
    flat = both.reshape(local_cells, 4, energies_dev, orbitals * orbitals)
    spread = lax.all_to_all(flat, "energy", split_axis=3, concat_axis=2, tiled=True)
    polar = correlate_spectral(spread).astype(jnp.bfloat16)
    polar_local = lax.all_to_all(polar, "energy", split_axis=2, concat_axis=3, tiled=True)
    sources = polar_local.reshape(local_cells, 2, energies_dev, orbitals, orbitals)
    sources = jnp.transpose(sources, (1, 2, 3, 0, 4)).reshape(
        2, energies_dev, orbitals, local_cells * orbitals
    )
    screened = lax.psum_scatter(
        sandwich_rows(
            w_screened, sources, coupling, cell_index, local_cells * lax.axis_size("cell")
        ).astype(jnp.bfloat16),
        "cell",
        scatter_dimension=0,
        tiled=True,
    )
    return (polar_local, screened)


def solution(mesh):
    return jax.shard_map(
        on_device,
        mesh=mesh,
        in_specs=(
            P(None, "energy", None, None, "cell"),
            P(None, "energy", None, "cell"),
            P(None, "energy", None, None, "cell"),
            P(),
        ),
        out_specs=(P("cell", None, "energy", None), P("cell", None, "energy", None, None)),
        check_vma=False,
    )
```

profile of v0, /device:TPU:0, one launch (start us, length us, event | category | flops | bytes accessed | tf_op | source)
XLA Modules:
  0.0 264.8 jit_solution(17689031934140179815)
XLA Ops:
  7.2 1.1 fusion.61
  8.3 1.1 fusion.65
  9.5 0.9 fusion.127
  10.4 1.1 fusion.31
  11.5 1.1 fusion.59
  12.6 1.1 fusion.29
  13.8 1.1 fusion.63
  14.9 1.1 fusion.24
  16.1 1.1 fusion.25
  17.2 0.7 pad_maximum_fusion
  18.0 0.9 constant_dynamic-slice_fusion.1
  19.4 1.2 dynamic-slice
  20.6 35.8 %all-reduce.5.cloned.1.call-done = bf16[4,2,1,128,128]{4,3,0,2,1:T(8,128)(2,1)} async-done(((bf16[4,2,1,128,128]{4,3,0,2,1:T(8,128)(2,1)}), bf16[4,2,1,128,128]{4,3,0,2,1:T(8,128)(2,1)}) %all-reduce.5.cloned.1.call-update) | async-done | bytes 262160
  56.4 1.5 fusion.36
  58.2 12.9 %copy.76 = bf16[1,4,1,16384]{1,2,0,3:T(2,128)(2,1)} copy(bf16[1,4,1,16384]{3,1,2,0:T(4,128)(2,1)S(1)} %pad_maximum_fusion.2) | data formatting | bytes 262144 | tf_op jit(solution)/shard_map/concatenate | solution.py:99
  71.0 0.5 broadcast.79
  71.6 90.8 %reduce.6 = bf16[16384,4]{1,0:T(8,128)(2,1)} reduce(bf16[16384,1,1,4]{3,2,1,0:T(2,128)(2,1)} %bitcast.233, bf16[]{:T(256)} %broadcast.79), dimensions={1,2}, to_apply=%bitcast.220.reduce_sub_computation | reduce | bytes 262146
  162.3 8.7 %reshape.445 = bf16[8,2,4096]{2,1,0:T(2,128)(2,1)S(1)} reshape(bf16[16384,4]{1,0:T(8,128)(2,1)} %reduce.6) | data formatting | bytes 262144
  171.0 9.0 %all_to_all.24 = bf16[8,2,4096]{2,1,0:T(2,128)(2,1)S(1)} all-to-all(bf16[8,2,4096]{2,1,0:T(2,128)(2,1)S(1)} %reshape.445), channel_id=1, replica_groups=mesh['energy'=8,'cell'=4] {'energy'}, dimensions={0} | all-to-all | bytes 262144 | tf_op jit(solution)/shard_map/all_to_all | solution.py:101
  180.0 11.1 %reshape.446 = bf16[16384,1,1,4]{3,2,1,0:T(2,128)(2,1)} reshape(bf16[8,2,4096]{2,1,0:T(2,128)(2,1)S(1)} %all_to_all.24) | data formatting | bytes 262144
  191.1 15.4 %copy.77 = bf16[1,4,1,16384]{3,1,2,0:T(4,128)(2,1)S(1)} copy(bf16[1,4,1,16384]{1,2,0,3:T(2,128)(2,1)} %bitcast.234) | data formatting | bytes 262144 | tf_op jit(solution)/shard_map/all_to_all | solution.py:101
  207.0 0.2 fusion.99
  207.4 0.2 fusion.104
  207.8 0.2 fusion.100
  208.2 0.2 convolution_add_fusion.1
  208.6 0.2 convolution_add_fusion.5
  208.8 0.2 convolution_add_fusion.7
  209.2 0.2 fusion.2
  209.4 0.2 fusion.3
  209.6 0.2 multiply_subtract_fusion
  209.8 0.3 fusion.50
  210.1 0.3 fusion.52
  210.4 0.3 fusion.11
  210.7 0.3 fusion.10
  211.0 7.4 %all_to_all.25 = bf16[1,2,8,2048]{3,1,0,2:T(2,128)(2,1)S(1)} all-to-all(bf16[1,2,8,2048]{3,1,0,2:T(2,128)(2,1)S(1)} %copy.78), channel_id=1, replica_groups=mesh['energy'=8,'cell'=4] {'energy'}, dimensions={2} | all-to-all | bytes 131072 | tf_op jit(solution)/shard_map/all_to_all | solution.py:103
  218.4 0.3 slice_reduce_fusion.1
  218.8 0.2 fusion.43
  219.0 0.2 fusion.47
  219.2 0.2 fusion.35
  219.4 0.2 fusion.33
  219.6 0.2 fusion.45
  219.9 0.2 fusion.41
  220.1 0.2 fusion.21
  220.4 0.2 fusion.20
  220.6 0.7 pad_maximum_fusion.1
  221.4 33.8 %all-reduce.7.cloned.1.call-done = bf16[4,2,1,128,128]{4,3,0,2,1:T(8,128)(2,1)} async-done(((bf16[4,2,1,128,128]{4,3,0,2,1:T(8,128)(2,1)}), bf16[4,2,1,128,128]{4,3,0,2,1:T(8,128)(2,1)}) %all-reduce.7.cloned.1.call-update) | async-done | bytes 262160
  255.2 2.1 dynamic-slice_bitcast_fusion
  257.3 0.6 copy.117
  (29 shorter events, 2.3 us)
Async XLA Ops:
  7.2 49.3 %all-reduce.5.cloned.1.call-start = ((), (), s32[]{:S(2)}) async-start(), calls=%async_computation.2 | async-start | bytes 524288
  18.0 237.2 %all-reduce.7.cloned.1.call-start = ((), (), s32[]{:S(2)}) async-start(), calls=%async_computation.3 | async-start | bytes 524288
  191.1 27.7 %copy-start = (bf16[2,1,4,128,128]{4,3,2,1,0:T(8,128)(2,1)S(1)}, bf16[2,1,4,128,128]{4,3,2,1,0:T(8,128)(2,1)}, u32[]{:S(2)}) copy-start(bf16[2,1,4,128,128]{4,3,2,1,0:T(8,128)(2,1)} %param.6) | copy-start | bytes 786436
Sparse Core Ops, SparseCore 0:
  18.1 38.2 all-reduce.4
  221.5 33.6 all-reduce.6
where the time goes:
time: 266 us; the launch traced here: 265 us
  other arithmetic  94.8 us (36%)
  waiting for transfers between devices  69.6 us (26%)
  local copies, waits for them, and re-layouts  54.4 us (20%)
  blocking collectives  16.4 us (6%)
  matrix products  15.2 us (6%)
  between operations  14.4 us (5%)
    unnamed x1, other arithmetic  90.8 us
    unnamed x4, waiting for transfers between devices  69.6 us
    unnamed x10, local copies, waits for them, and re-layouts  24.5 us
    all_to_all x1, local copies, waits for them, and re-layouts, on_device(): lax.all_to_all(flat, 'energy', split_axis=3, concat_axis=2, tiled=True)  15.4 us
    concatenate x3, local copies, waits for them, and re-layouts, on_device(): both = jnp.concatenate([lesser, greater], axis=1).astype(jnp.bfloat16)  12.9 us
    all_to_all x1, blocking collectives, on_device(): lax.all_to_all(flat, 'energy', split_axis=3, concat_axis=2, tiled=True)  8.95 us
    all_to_all x1, blocking collectives, on_device(): lax.all_to_all(polar, 'energy', split_axis=2, concat_axis=3, tiled=True)  7.4 us
    dot_general x8, matrix products, adjoint_product(): jnp.einsum('eibjc,eidjc->iebd', left, right, preferred_element_type=jnp.f...  5.52 us
  transfers between devices with their start and end apart: 2, of which 2 were waited for; matrix products, arithmetic and copies ran while one was open for 1% of the time, Pallas kernels for 0%

commit v1 on v0

--- a/solution.py
+++ b/solution.py
@@ -98,7 +98,16 @@
     )
     both = jnp.concatenate([lesser, greater], axis=1).astype(jnp.bfloat16)
     flat = both.reshape(local_cells, 4, energies_dev, orbitals * orbitals)
-    spread = lax.all_to_all(flat, "energy", split_axis=3, concat_axis=2, tiled=True)
+    try_all_cubes_on_mesh = lambda mine_x, a_name: jnp.concatenate(
+        lax.all_to_all(
+            jnp.stack(jnp.split(mine_x, lax.axis_size(a_name), 3), axis=0),
+            split_axis=0,
+            axis_name=a_name,
+            concat_axis=0,
+        ),
+        2,
+    )
+    spread = try_all_cubes_on_mesh(flat, "energy")
     polar = correlate_spectral(spread).astype(jnp.bfloat16)
     polar_local = lax.all_to_all(polar, "energy", split_axis=2, concat_axis=3, tiled=True)
     sources = polar_local.reshape(local_cells, 2, energies_dev, orbitals, orbitals)

time: 266 us -> 120 us (0.45)
  other arithmetic: 94.8 us -> 3.43 us
  local copies, waits for them, and re-layouts: 54.4 us -> 5.83 us
  matrix products: 15.2 us -> 8.77 us
    unnamed x1 -> x7, other arithmetic: 90.8 us -> 0.22 us
    unnamed x10 -> x18, local copies, waits for them, and re-layouts: 24.5 us -> 4.9 us
    all_to_all x1 -> x0, local copies, waits for them, and re-layouts: 15.4 us -> none  [on_device(): lax.all_to_all(flat, 'energy', split_axis=3, concat_axis=2, tiled=True)]
    concatenate x3 -> x2, local copies, waits for them, and re-layouts: 12.9 us -> 0.04 us  [on_device(): both = jnp.concatenate([lesser, greater], axis=1).astype(jnp.bfloat16)]
    dot_general x8, matrix products: 5.52 us -> 1.9 us  [adjoint_product(): jnp.einsum('eibjc,eidjc->iebd', left, right, preferred_element_type=jnp.f...]
    dot_general x8, matrix products: 5.35 us -> 2.62 us  [forward_product(): jnp.einsum('eibjc,ecjd->eibjd', left, right, preferred_element_type=jnp.f...]
where the time goes in v1:
time: 120 us
  waiting for transfers between devices  70.5 us (59%)
  blocking collectives  16.5 us (14%)
  between operations  14.4 us (12%)
  matrix products  8.77 us (7%)
  local copies, waits for them, and re-layouts  5.83 us (5%)
  other arithmetic  3.43 us (3%)
    unnamed x4, waiting for transfers between devices  70.5 us
    all_to_all x1, blocking collectives, on_device(): lax.all_to_all(jnp.stack(jnp.split(mine_x, lax.axis_size(a_name), 3), axi...  8.95 us
    all_to_all x1, blocking collectives, on_device(): lax.all_to_all(polar, 'energy', split_axis=2, concat_axis=3, tiled=True)  7.53 us
    unnamed x18, local copies, waits for them, and re-layouts  4.9 us
    dot_general x8, matrix products, forward_product(): jnp.einsum('eibjc,ecjd->eibjd', left, right, preferred_element_type=jnp.f...  2.62 us
  transfers between devices with their start and end apart: 2, of which 2 were waited for; matrix products, arithmetic and copies ran while one was open for 1% of the time, Pallas kernels for 0%

profile of v1, /device:TPU:0, one launch (start us, length us, event | category | flops | bytes accessed | tf_op | source)
XLA Modules:
  0.0 119.5 jit_solution(8124895543061045879)
XLA Ops:
  7.2 1.2 fusion.61
  8.4 0.2 fusion.65
  8.6 0.7 copy-done.3
  9.5 0.2 fusion.31
  9.7 0.2 fusion.59
  10.0 0.2 fusion.29
  10.2 0.2 fusion.63
  10.4 0.2 fusion.24
  10.7 0.2 fusion.25
  10.9 0.7 pad_maximum_fusion
  12.2 0.6 copy-done.4
  12.9 0.6 dynamic-slice
  13.5 36.7 %all-reduce.5.cloned.1.call-done = bf16[4,2,1,128,128]{4,3,0,2,1:T(8,128)(2,1)} async-done(((bf16[4,2,1,128,128]{4,3,0,2,1:T(8,128)(2,1)}), bf16[4,2,1,128,128]{4,3,0,2,1:T(8,128)(2,1)}) %all-reduce.5.cloned.1.call-update) | async-done | bytes 262160
  50.1 1.5 %fusion.36 = (bf16[1,2,1,128,128]{4,3,0,2,1:T(8,128)(2,1)S(1)}, bf16[1,2,1,128,128]{4,3,0,2,1:T(8,128)(2,1)S(1)}) fusion(f32[1,1,1,128,128]{4,3,0,2,1:T(8,128)S(1)} %fusion.83, f32[1,1,1,128,128]{4,3,0,2,1:T(8,128)S(1)} %copy.95, bf16[4,2,1,128,128]{4,3,0,2,1:T(8,128)(2,1)} %all-reduce.5.cloned.1.call-done, u32[]{:T(128)} %bitcast.83), kind=kLoop, calls=%fused_computation.71 | loop fusion | flops 131072 | bytes 327684 | tf_op jit(solution)/shard_map/convert.14
  52.0 8.9 %all_to_all.17 = bf16[8,1,4,1,2048]{4,2,3,1,0:T(4,128)(2,1)S(1)} all-to-all(bf16[8,1,4,1,2048]{4,2,3,1,0:T(4,128)(2,1)S(1)} %constant_dynamic-update-slice_fusion), channel_id=1, replica_groups=mesh['energy'=8,'cell'=4] {'energy'}, dimensions={0} | all-to-all | bytes 262144 | tf_op jit(solution)/shard_map/all_to_all | solution.py:102
  60.9 0.2 fusion.232
  61.3 0.2 fusion.105
  61.6 0.2 fusion.93
  61.8 0.2 fusion.90
  62.0 0.2 fusion.99
  62.2 0.2 fusion.96
  62.6 0.2 fusion.108
  62.8 0.2 convolution_add_fusion.3
  63.0 0.2 convolution_add_fusion.5
  63.2 0.2 convolution_add_fusion.7
  63.4 0.2 convolution_add_fusion.1
  63.6 0.2 fusion.2
  63.8 0.2 fusion.3
  64.0 0.2 fusion
  64.2 0.2 multiply_subtract_fusion
  64.4 0.3 fusion.50
  64.7 0.3 fusion.52
  65.0 0.3 fusion.11
  65.3 0.3 fusion.10
  65.7 7.5 %all_to_all.18 = bf16[1,2,8,2048]{3,1,0,2:T(2,128)(2,1)S(1)} all-to-all(bf16[1,2,8,2048]{3,1,0,2:T(2,128)(2,1)S(1)} %copy.96), channel_id=1, replica_groups=mesh['energy'=8,'cell'=4] {'energy'}, dimensions={2} | all-to-all | bytes 131072 | tf_op jit(solution)/shard_map/all_to_all | solution.py:112
  73.2 0.3 slice_reduce_fusion.1
  73.5 0.2 fusion.47
  73.8 0.2 fusion.43
  74.0 0.2 fusion.33
  74.2 0.2 fusion.45
  74.4 0.2 fusion.35
  74.6 0.2 fusion.41
  74.9 0.2 fusion.21
  75.1 0.2 fusion.20
  75.4 0.7 pad_maximum_fusion.1
  76.1 33.8 %all-reduce.7.cloned.1.call-done = bf16[4,2,1,128,128]{4,3,0,2,1:T(8,128)(2,1)} async-done(((bf16[4,2,1,128,128]{4,3,0,2,1:T(8,128)(2,1)}), bf16[4,2,1,128,128]{4,3,0,2,1:T(8,128)(2,1)}) %all-reduce.7.cloned.1.call-update) | async-done | bytes 262160
  109.9 2.1 %dynamic-slice_bitcast_fusion = bf16[1,2,1,128,128]{4,3,2,1,0:T(8,128)(2,1)} fusion(bf16[4,2,1,128,128]{4,3,0,2,1:T(8,128)(2,1)} %all-reduce.7.cloned.1.call-done, u32[]{:T(128)} %bitcast.83), kind=kLoop, calls=%fused_computation.126 | loop fusion | bytes 131076
  112.1 0.6 copy.143
  (42 shorter events, 1.7 us)
Async XLA Ops:
  7.2 1.2 %copy-start = (bf16[2,1,4,128,128]{4,3,2,1,0:T(8,128)(2,1)S(1)}, bf16[2,1,4,128,128]{4,3,2,1,0:T(8,128)(2,1)}, u32[]{:S(2)}) copy-start(bf16[2,1,4,128,128]{4,3,2,1,0:T(8,128)(2,1)} %param.4) | copy-start | bytes 786436
  7.2 43.0 %all-reduce.5.cloned.1.call-start = ((), (), s32[]{:S(2)}) async-start(), calls=%async_computation.2 | async-start | bytes 524288
  7.2 1.2 copy-start.2
  8.6 0.7 copy-start.3
  11.7 98.3 %all-reduce.7.cloned.1.call-start = ((), (), s32[]{:S(2)}) async-start(), calls=%async_computation.3 | async-start | bytes 524288
  12.2 0.7 copy-start.4
  65.7 7.9 %copy-start.1 = (bf16[2,1,4,128,128]{4,3,2,1,0:T(8,128)(2,1)S(1)}, bf16[2,1,4,128,128]{4,3,2,1,0:T(8,128)(2,1)}, u32[]{:S(2)}) copy-start(bf16[2,1,4,128,128]{4,3,2,1,0:T(8,128)(2,1)} %param.6) | copy-start | bytes 786436
Sparse Core Ops, SparseCore 0:
  11.8 38.3 all-reduce.4
  76.2 33.6 all-reduce.6
